TPU v7x, 32 devices: a whole 2x2x4 slice. The times are simulated.
32 devices in a mesh: row: 4 (over y, core), col: 4 (over z), layer: 2 (over x).
Axes of the slice: x: 2, y: 2, z: 4, core: 2. Of those that a mesh axis runs over, the one named last changes fastest.
Arguments:
- hamiltonian: bfloat16 [2560, 2560], P(('row', 'layer'), 'col'), may hold values from -1.2 to 1.2, as said below
- tile_pattern: int32 [20, 20], replicated, may hold values from 0 to 1, as said below
- n_occ: int32 [1], replicated, may hold values from 512 to 2047
- mu: float32 [1], replicated, may hold values from -0.2 to 0.2
- gamma: float32 [1], replicated, may hold values from 0.25 to 0.4
Outputs:
- density: float32 [2560, 2560], P(('row', 'layer'), 'col')
Inputs may be any that keep to these rules, and one draw needn't show every extreme that they name: `tile_pattern`: Symmetric, 0 or 1, with ones on the diagonal and next to it. `hamiltonian`: Symmetric; its eigenvalues lie within -1.8 and 1.8.
All inputs are finite; a program needn't handle non-finite values.
Results may differ from a plain program's by a relative error of at most 0.0055.
Values may be sent and summed in bfloat16 or wider, within the bound.
A program may use at most 64 MiB of HBM per device.

v0:
```python
import jax
import jax.numpy as jnp
from jax import lax
from jax.sharding import PartitionSpec as P

TILE = 128
STEPS = 2


def element_mask(tile_pattern, row_start, row_count, col_start, col_count):
    tile_count = tile_pattern.shape[0]
    tile_ids = jnp.arange(tile_count, dtype=jnp.int32)
    row_tiles = (row_start + jnp.arange(row_count, dtype=jnp.int32)) // TILE
    col_tiles = (col_start + jnp.arange(col_count, dtype=jnp.int32)) // TILE
    row_hot = (row_tiles[:, None] == tile_ids[None, :]).astype(jnp.bfloat16)
    col_hot = (tile_ids[:, None] == col_tiles[None, :]).astype(jnp.bfloat16)
    picked = jnp.dot(row_hot, tile_pattern.astype(jnp.bfloat16), preferred_element_type=jnp.float32)
    return jnp.dot(picked.astype(jnp.bfloat16), col_hot, preferred_element_type=jnp.float32)


def shards(hamiltonian, tile_pattern, n_occ, mu, gamma):
    share_rows, band_cols = hamiltonian.shape
    n_col = lax.axis_size("col")
    n_layer = lax.axis_size("layer")
    order = band_cols * n_col
    layer_index = lax.axis_index("layer")
    row_start = (lax.axis_index("row") * n_layer + layer_index) * share_rows
    col_start = lax.axis_index("col") * band_cols
    mask = element_mask(tile_pattern, row_start, share_rows, col_start, band_cols)
    row_global = row_start + jnp.arange(share_rows, dtype=jnp.int32)
    col_global = col_start + jnp.arange(band_cols, dtype=jnp.int32)
    identity = (row_global[:, None] == col_global[None, :]).astype(jnp.float32)
    filling = n_occ[0].astype(jnp.float32) / order
    start = mask * (
        filling * identity + gamma[0] * (mu[0] * identity - hamiltonian.astype(jnp.float32))
    )
    current = start.astype(jnp.bfloat16)
    result = start
    for iteration in range(STEPS):
        column = lax.all_gather(current, ("row", "layer"), axis=0, tiled=True)

        def rows_product(left_share):
            return jnp.dot(
                lax.all_gather(left_share, "col", axis=1, tiled=True),
                column,
                preferred_element_type=jnp.float32,
            )

        square = mask * rows_product(current)
        cube = mask * rows_product(square.astype(jnp.bfloat16))
        result = 3.0 * square - 2.0 * cube
        current = result.astype(jnp.bfloat16)
    return result


def solution(mesh):
    placed = (P(("row", "layer"), "col"), P(), P(), P(), P())
    return jax.shard_map(
        shards, mesh=mesh, in_specs=placed, out_specs=P(("row", "layer"), "col"), check_vma=False
    )
```

profile of v0, /device:TPU:6, one launch (start us, length us, event | category | flops | bytes accessed | tf_op | source)
XLA Modules:
  0.0 256.6 jit_solution(9682719077241152111)
XLA Ops:
  6.5 0.0 all-gather.7.cloned.1.call-start
  8.5 2.5 fusion.8
  11.0 0.0 all-gather.7.cloned.1.call-update
  11.1 0.0 all-gather.9.cloned.1.call-start
  11.1 0.7 all-gather.9.cloned.1.call-update
  11.8 0.0 all-gather.11.cloned.1.call-start
  11.9 38.4 %all-gather.7.cloned.1.call-done = bf16[320,2560]{1,0:T(8,128)(2,1)} async-done(((bf16[320,640]{1,0:T(8,128)(2,1)}), bf16[320,2560]{1,0:T(8,128)(2,1)}) %all-gather.7.cloned.1.call-update) | async-done | bytes 1638416 | tf_op jit(solution)/shard_map/all_gather | solution.py:44
  50.3 32.8 %all-gather.9.cloned.1.call-done = bf16[2560,640]{1,0:T(8,128)(2,1)} async-done(((bf16[320,640]{1,0:T(8,128)(2,1)}), bf16[2560,640]{1,0:T(8,128)(2,1)}) %all-gather.9.cloned.1.call-update) | async-done | bytes 3276816 | tf_op jit(solution)/shard_map/all_gather | solution.py:40
  83.1 0.0 copy-start
  83.1 5.3 %fusion.24 = (bf16[320,640]{1,0:T(8,128)(2,1)}, f32[320,640]{1,0:T(8,128)}) fusion(f32[320,640]{1,0:T(8,128)} %get-tuple-element.6, bf16[320,2560]{1,0:T(8,128)(2,1)} %all-gather.7.cloned.1.call-done, bf16[2560,640]{1,0:T(8,128)(2,1)} %all-gather.9.cloned.1.call-done), kind=kOutput, calls=%fused_computation.41 | convolution fusion | flops 1048985600 | bytes 6963200 | tf_op jit(solution)/shard_map/dot_general | solution.py:43
  88.4 0.0 all-gather.11.cloned.1.call-update
  88.4 0.0 all-gather.13.cloned.1.call-start
  88.5 38.9 %all-gather.11.cloned.1.call-done = bf16[320,2560]{1,0:T(8,128)(2,1)} async-done(((bf16[320,640]{1,0:T(8,128)(2,1)}), bf16[320,2560]{1,0:T(8,128)(2,1)}) %all-gather.11.cloned.1.call-update) | async-done | bytes 1638416 | tf_op jit(solution)/shard_map/all_gather | solution.py:44
  127.4 0.0 copy-done
  127.4 4.1 %fusion.4 = bf16[320,640]{1,0:T(8,128)(2,1)} fusion(f32[320,640]{1,0:T(8,128)} %get-tuple-element.6, bf16[320,2560]{1,0:T(8,128)(2,1)} %all-gather.11.cloned.1.call-done, bf16[2560,640]{1,0:T(8,128)(2,1)S(1)} %copy-done, f32[320,640]{1,0:T(8,128)} %get-tuple-element.8), kind=kOutput, calls=%fused_computation.8 | convolution fusion | flops 1049600000 | bytes 6963200 | tf_op jit(solution)/shard_map/dot_general | solution.py:43
  131.5 0.0 all-gather.13.cloned.1.call-update
  131.5 0.0 all-gather.15.cloned.1.call-start
  131.5 0.5 all-gather.15.cloned.1.call-update
  132.1 0.0 all-gather.17.cloned.1.call-start
  132.1 36.5 %all-gather.13.cloned.1.call-done = bf16[320,2560]{1,0:T(8,128)(2,1)} async-done(((bf16[320,640]{1,0:T(8,128)(2,1)}), bf16[320,2560]{1,0:T(8,128)(2,1)}) %all-gather.13.cloned.1.call-update) | async-done | bytes 1638416 | tf_op jit(solution)/shard_map/all_gather | solution.py:44
  168.6 32.7 %all-gather.15.cloned.1.call-done = bf16[2560,640]{1,0:T(8,128)(2,1)} async-done(((bf16[320,640]{1,0:T(8,128)(2,1)}), bf16[2560,640]{1,0:T(8,128)(2,1)}) %all-gather.15.cloned.1.call-update) | async-done | bytes 3276816 | tf_op jit(solution)/shard_map/all_gather | solution.py:40
  201.3 0.0 copy-start.1
  201.3 5.3 %fusion.25 = (bf16[320,640]{1,0:T(8,128)(2,1)}, f32[320,640]{1,0:T(8,128)}) fusion(f32[320,640]{1,0:T(8,128)} %get-tuple-element.6, bf16[320,2560]{1,0:T(8,128)(2,1)} %all-gather.13.cloned.1.call-done, bf16[2560,640]{1,0:T(8,128)(2,1)} %all-gather.15.cloned.1.call-done), kind=kOutput, calls=%fused_computation.42 | convolution fusion | flops 1048985600 | bytes 6963200 | tf_op jit(solution)/shard_map/dot_general | solution.py:43
  206.6 0.0 all-gather.17.cloned.1.call-update
  206.6 39.0 %all-gather.17.cloned.1.call-done = bf16[320,2560]{1,0:T(8,128)(2,1)} async-done(((bf16[320,640]{1,0:T(8,128)(2,1)}), bf16[320,2560]{1,0:T(8,128)(2,1)}) %all-gather.17.cloned.1.call-update) | async-done | bytes 1638416 | tf_op jit(solution)/shard_map/all_gather | solution.py:44
  245.6 0.0 copy-done.1
  245.6 4.2 %fusion.3 = f32[320,640]{1,0:T(8,128)} fusion(f32[320,640]{1,0:T(8,128)} %get-tuple-element.6, bf16[320,2560]{1,0:T(8,128)(2,1)} %all-gather.17.cloned.1.call-done, bf16[2560,640]{1,0:T(8,128)(2,1)S(1)} %copy-done.1, f32[320,640]{1,0:T(8,128)} %get-tuple-element.10), kind=kOutput, calls=%fused_computation.7 | convolution fusion | flops 1049395200 | bytes 7372800 | tf_op jit(solution)/shard_map/dot_general | solution.py:43
  (2 shorter events, 0.0 us)
Async XLA Ops:
  6.5 43.7 %all-gather.7.cloned.1.call-start = ((), (), s32[]{:S(2)}) async-start(), calls=%async_computation | async-start | bytes 2048000 | tf_op jit(solution)/shard_map/all_gather | solution.py:44
  11.1 72.1 %all-gather.9.cloned.1.call-start = ((), (), s32[]{:S(2)}) async-start(), calls=%async_computation.1 | async-start | bytes 3686400 | tf_op jit(solution)/shard_map/all_gather | solution.py:40
  11.8 115.6 %all-gather.11.cloned.1.call-start = ((), (), s32[]{:S(2)}) async-start(), calls=%async_computation.2 | async-start | bytes 2048000 | tf_op jit(solution)/shard_map/all_gather | solution.py:44
  83.1 44.3 %copy-start = (bf16[2560,640]{1,0:T(8,128)(2,1)S(1)}, bf16[2560,640]{1,0:T(8,128)(2,1)}, u32[]{:S(2)}) copy-start(bf16[2560,640]{1,0:T(8,128)(2,1)} %all-gather.9.cloned.1.call-done) | copy-start | bytes 9830404
  88.4 80.2 %all-gather.13.cloned.1.call-start = ((), (), s32[]{:S(2)}) async-start(), calls=%async_computation.3 | async-start | bytes 2048000 | tf_op jit(solution)/shard_map/all_gather | solution.py:44
  131.5 69.8 %all-gather.15.cloned.1.call-start = ((), (), s32[]{:S(2)}) async-start(), calls=%async_computation.4 | async-start | bytes 3686400 | tf_op jit(solution)/shard_map/all_gather | solution.py:40
  132.1 113.5 %all-gather.17.cloned.1.call-start = ((), (), s32[]{:S(2)}) async-start(), calls=%async_computation.5 | async-start | bytes 2048000 | tf_op jit(solution)/shard_map/all_gather | solution.py:44
  201.3 44.3 %copy-start.1 = (bf16[2560,640]{1,0:T(8,128)(2,1)S(1)}, bf16[2560,640]{1,0:T(8,128)(2,1)}, u32[]{:S(2)}) copy-start(bf16[2560,640]{1,0:T(8,128)(2,1)} %all-gather.15.cloned.1.call-done) | copy-start | bytes 9830404
Sparse Core Ops, SparseCore 0:
  11.2 39.0 all-gather.6
  52.2 30.9 all-gather.8
  88.5 38.7 all-gather.10
  131.6 36.9 all-gather.12
  170.4 30.9 all-gather.14
  206.8 38.7 all-gather.16
where the time goes:
time: 258 us; the launch traced here: 257 us
  waiting for transfers between devices  220 us (85%)
  matrix products  21.3 us (8%)
  between operations  15.4 us (6%)
    all_gather x4, waiting for transfers between devices, rows_product(): lax.all_gather(left_share, 'col', axis=1, tiled=True)  153 us
    all_gather x2, waiting for transfers between devices, shards(): column = lax.all_gather(current, ('row', 'layer'), axis=0, tiled=True)  65.5 us
    dot_general x4, matrix products, rows_product(): jnp.dot(lax.all_gather(left_share, 'col', axis=1, tiled=True), column, pr...  18.8 us
  transfers between devices with their start and end apart: 6, of which 6 were waited for; matrix products, arithmetic and copies ran while one was open for 0% of the time, Pallas kernels for 0%

commit v1 on v0

--- a/solution.py
+++ b/solution.py
@@ -1,6 +1,10 @@
+import functools
+
 import jax
 import jax.numpy as jnp
 from jax import lax
+from jax.experimental import pallas as pl
+from jax.experimental.pallas import tpu as pltpu
 from jax.sharding import PartitionSpec as P
 
 TILE = 128
@@ -18,7 +22,7 @@
     return jnp.dot(picked.astype(jnp.bfloat16), col_hot, preferred_element_type=jnp.float32)
 
 
-def shards(hamiltonian, tile_pattern, n_occ, mu, gamma):
+def plain_shards(hamiltonian, tile_pattern, n_occ, mu, gamma):
     share_rows, band_cols = hamiltonian.shape
     n_col = lax.axis_size("col")
     n_layer = lax.axis_size("layer")
@@ -53,6 +57,293 @@
     return result
 
 
+F32 = jnp.float32
+BF16 = jnp.bfloat16
+Z_UP, Z_DOWN, L_UP, L_DOWN, TO_Y, TO_CORE = range(6)
+
+
+def kernel(sizes, cur, flags, out, full, square, half, half2, strip, column, send1, recv1, send2, recv2, send3, recv3):
+    n_row, n_col, n_layer, bm, bn = sizes
+    order = bn * n_col
+    half_order = order // 2
+    bands = n_col // 2
+    row, z, layer = lax.axis_index("row"), lax.axis_index("col"), lax.axis_index("layer")
+    y, core = row // 2, row % 2
+    row_y = (1 - y) * 2 + core
+    row_c = y * 2 + 1 - core
+    row_yc = (1 - y) * 2 + 1 - core
+
+    barrier = pltpu.get_barrier_semaphore()
+
+    def greet(cond, device):
+        @pl.when(cond)
+        def _():
+            pl.semaphore_signal(barrier, inc=1, device_id=device, device_id_type=pl.DeviceIdType.MESH)
+
+    neighbours = [
+        (z > 0, {"col": z - 1}),
+        (z < n_col - 1, {"col": z + 1}),
+        (layer > 0, {"layer": layer - 1}),
+        (layer < n_layer - 1, {"layer": layer + 1}),
+    ]
+    for cond, device in neighbours:
+        greet(cond, device)
+    for device in ({"row": row_y}, {"row": row_c}):
+        pl.semaphore_signal(barrier, inc=1, device_id=device, device_id_type=pl.DeviceIdType.MESH)
+    peers = 2
+    for cond, _device in neighbours:
+        peers = peers + jnp.where(cond, 1, 0)
+    pl.semaphore_wait(barrier, peers)
+
+    def rows_of(r, l):
+        return pl.ds(pl.multiple_of((r * n_layer + l) * bm, bm), bm)
+
+    def cols_of(b):
+        return pl.ds(pl.multiple_of(b * bn, bn), bn)
+
+    def always(cond, body):
+        if cond is None:
+            body()
+        else:
+            pl.when(cond)(body)
+
+    def both(a, b):
+        if a is None:
+            return b
+        if b is None:
+            return a
+        return jnp.logical_and(a, b)
+
+    class Gather:
+        def __init__(self, view, index, send, recv):
+            self.view, self.index, self.send, self.recv = view, index, send, recv
+            self.pending = []
+
+        def copy(self, way, block, device, src=None):
+            dst = self.view(*block)
+            at = self.index(*block)
+            return pltpu.make_async_remote_copy(
+                src_ref=dst if src is None else src,
+                dst_ref=dst,
+                send_sem=self.send.at[way, at],
+                recv_sem=self.recv.at[at],
+                device_id=device,
+                device_id_type=pl.DeviceIdType.MESH,
+            )
+
+        def start(self, cond, way, block, device, src=None):
+            always(cond, lambda: self.copy(way, block, device, src).start())
+            self.pending.append((cond, way, block, device, src))
+
+        def arrive(self, cond, block):
+            always(cond, lambda: self.copy(TO_CORE, block, {"row": row_c}).wait_recv())
+
+        def drain(self):
+            for cond, way, block, device, src in self.pending:
+                always(cond, lambda: self.copy(way, block, device, src).wait_send())
+
+    g = Gather(
+        lambda r, l, b: full.at[rows_of(r, l), cols_of(b)],
+        lambda r, l, b: (r * n_layer + l) * n_col + b,
+        send1,
+        recv1,
+    )
+
+    def spread(cond, block, up, down, src=None):
+        r, l, b = block
+        if up:
+            g.start(both(cond, layer < n_layer - 1), L_UP, block, {"layer": layer + 1}, src)
+        if down:
+            g.start(both(cond, layer > 0), L_DOWN, block, {"layer": layer - 1}, src)
+        g.start(both(cond, b // bands == y), TO_Y, block, {"row": row_y}, src)
+        g.start(cond, TO_CORE, block, {"row": row_c}, src)
+
+    mine = (row, layer, z)
+    g.start(z < n_col - 1, Z_UP, mine, {"col": z + 1}, cur)
+    g.start(z > 0, Z_DOWN, mine, {"col": z - 1}, cur)
+    spread(None, mine, True, True, cur)
+    full[rows_of(row, layer), cols_of(z)] = cur[...]
+
+    def layer_arrivals(cond, b):
+        for e in range(1, n_layer):
+            for sign in (-1, 1):
+                l = layer + sign * e
+                inside = both(cond, l >= 0 if sign < 0 else l < n_layer)
+                g.arrive(inside, (row, l, b))
+                spread(inside, (row, l, b), sign < 0, sign > 0)
+
+    for d in range(1, n_col):
+        for sign in (-1, 1):
+            b = z + sign * d
+            inside = b >= 0 if sign < 0 else b < n_col
+            block = (row, layer, b)
+            g.arrive(inside, block)
+            if sign < 0:
+                g.start(both(inside, z < n_col - 1), Z_UP, block, {"col": z + 1})
+            else:
+                g.start(both(inside, z > 0), Z_DOWN, block, {"col": z - 1})
+            spread(inside, block, True, True)
+        if d == 1:
+            layer_arrivals(None, z)
+        else:
+            layer_arrivals(z - d + 1 >= 0, z - d + 1)
+            layer_arrivals(z + d - 1 < n_col, z + d - 1)
+    layer_arrivals(z - n_col + 1 >= 0, z - n_col + 1)
+    layer_arrivals(z + n_col - 1 < n_col, z + n_col - 1)
+    for b in range(bands):
+        for l in range(n_layer):
+            block = (row_y, l, (1 - y) * bands + b)
+            g.arrive(None, block)
+            g.start(None, TO_CORE, block, {"row": row_c})
+    for l in range(n_layer):
+        for b in range(n_col):
+            g.arrive(None, (row_c, l, b))
+        for b in range(bands):
+            g.arrive(None, (row_yc, l, (1 - y) * bands + b))
+    g.drain()
+
+    mine_at = pl.multiple_of(y * half_order, half_order)
+    other_at = pl.multiple_of((1 - y) * half_order, half_order)
+
+    @pl.loop(0, half_order // TILE)
+    def _(t):
+        here = pl.ds(pl.multiple_of(mine_at + t * TILE, TILE), TILE)
+        full[pl.ds(other_at, half_order), here] = full[here, pl.ds(other_at, half_order)].T
+
+    own_rows = rows_of(row, layer)
+
+    def mask_of(b):
+        tiles = flags.shape[1]
+        tile = lax.broadcasted_iota(jnp.int32, (tiles, bn), 0)
+        column_tile = (b * bn + lax.broadcasted_iota(jnp.int32, (tiles, bn), 1)) // TILE
+        return jnp.dot(flags[...], (tile == column_tile).astype(BF16), preferred_element_type=F32)
+
+    @pl.loop(0, n_col)
+    def _(b):
+        value = mask_of(b) * jnp.dot(full[own_rows, :], full[:, cols_of(b)], preferred_element_type=F32)
+        square[:, cols_of(b)] = value
+        half[:, cols_of(b)] = value.astype(BF16)
+
+    c = Gather(
+        lambda r, l: column.at[rows_of(r, l), :],
+        lambda r, l: r * n_layer + l,
+        send2,
+        recv2,
+    )
+
+    def cube_band(b):
+        cube = mask_of(b) * jnp.dot(half[...], full[:, cols_of(b)], preferred_element_type=F32)
+        return (3.0 * square[:, cols_of(b)] - 2.0 * cube).astype(BF16)
+
+    def spread_column(cond, block, up, down):
+        if up:
+            c.start(both(cond, layer < n_layer - 1), L_UP, block, {"layer": layer + 1})
+        if down:
+            c.start(both(cond, layer > 0), L_DOWN, block, {"layer": layer - 1})
+        c.start(cond, TO_Y, block, {"row": row_y})
+        c.start(cond, TO_CORE, block, {"row": row_c})
+
+    first = cube_band(z)
+    column[own_rows, :] = first
+    strip[:, cols_of(z)] = first
+    spread_column(None, (row, layer), True, True)
+
+    @pl.loop(1, n_col)
+    def _(i):
+        b = lax.rem(z + i, n_col)
+        strip[:, cols_of(b)] = cube_band(b)
+
+    for e in range(1, n_layer):
+        for sign in (-1, 1):
+            l = layer + sign * e
+            inside = l >= 0 if sign < 0 else l < n_layer
+            c.arrive(inside, (row, l))
+            spread_column(inside, (row, l), sign < 0, sign > 0)
+    for l in range(n_layer):
+        c.arrive(None, (row_y, l))
+        c.start(None, TO_CORE, (row_y, l), {"row": row_c})
+    for l in range(n_layer):
+        c.arrive(None, (row_c, l))
+    for l in range(n_layer):
+        c.arrive(None, (row_yc, l))
+
+    mask_z = mask_of(z)
+    last = mask_z * jnp.dot(strip[...], column[...], preferred_element_type=F32)
+    out[...] = 3.0 * last
+    half2[:, cols_of(z)] = last.astype(BF16)
+    s = Gather(lambda b: half2.at[:, cols_of(b)], lambda b: b, send3, recv3)
+    s.start(z < n_col - 1, Z_UP, (z,), {"col": z + 1})
+    s.start(z > 0, Z_DOWN, (z,), {"col": z - 1})
+
+    def cube_part(b):
+        part = jnp.dot(half2[:, cols_of(b)], column[cols_of(b), :], preferred_element_type=F32)
+        out[...] -= (2.0 * mask_z) * part
+
+    cube_part(z)
+    for d in range(1, n_col):
+        for sign in (-1, 1):
+            b = z + sign * d
+            inside = b >= 0 if sign < 0 else b < n_col
+            s.arrive(inside, (b,))
+            if sign < 0:
+                s.start(both(inside, z < n_col - 1), Z_UP, (b,), {"col": z + 1})
+            else:
+                s.start(both(inside, z > 0), Z_DOWN, (b,), {"col": z - 1})
+        for sign in (-1, 1):
+            b = z + sign * d
+            inside = b >= 0 if sign < 0 else b < n_col
+            always(inside, functools.partial(cube_part, b))
+    s.drain()
+    c.drain()
+
+
+def shards(hamiltonian, tile_pattern, n_occ, mu, gamma):
+    bm, bn = hamiltonian.shape
+    n_row, n_col, n_layer = (lax.axis_size(a) for a in ("row", "col", "layer"))
+    order = bn * n_col
+    vmem = 2 * order * (order + 3 * bm + bn) + 4 * bm * (order + bn) + 2 * bm * bn
+    regular = n_row == 4 and n_col % 2 == 0 and n_layer * bm * n_row == order
+    aligned = bm % 16 == 0 and bn % TILE == 0 and (order // 2) % TILE == 0
+    if not (regular and aligned and vmem <= 48 << 20):
+        return plain_shards(hamiltonian, tile_pattern, n_occ, mu, gamma)
+    row_start = (lax.axis_index("row") * n_layer + lax.axis_index("layer")) * bm
+    col_start = lax.axis_index("col") * bn
+    rows = row_start + jnp.arange(bm, dtype=jnp.int32)
+    cols = col_start + jnp.arange(bn, dtype=jnp.int32)
+    tile_ids = jnp.arange(tile_pattern.shape[0], dtype=jnp.int32)
+    row_hot = (rows[:, None] // TILE == tile_ids[None, :]).astype(BF16)
+    flags = jnp.dot(row_hot, tile_pattern.astype(BF16), preferred_element_type=F32).astype(BF16)
+    col_hot = (tile_ids[:, None] == cols[None, :] // TILE).astype(BF16)
+    mask = jnp.dot(flags, col_hot, preferred_element_type=F32)
+    identity = (rows[:, None] == cols[None, :]).astype(F32)
+    filling = n_occ[0].astype(F32) / order
+    start = mask * (filling * identity + gamma[0] * (mu[0] * identity - hamiltonian.astype(F32)))
+    blocks = n_row * n_layer
+    return pl.pallas_call(
+        functools.partial(kernel, (n_row, n_col, n_layer, bm, bn)),
+        out_shape=jax.ShapeDtypeStruct((bm, bn), F32),
+        in_specs=[pl.BlockSpec(memory_space=pltpu.VMEM)] * 2,
+        out_specs=pl.BlockSpec(memory_space=pltpu.VMEM),
+        scratch_shapes=[
+            pltpu.VMEM((order, order), BF16),
+            pltpu.VMEM((bm, order), F32),
+            pltpu.VMEM((bm, order), BF16),
+            pltpu.VMEM((bm, order), BF16),
+            pltpu.VMEM((bm, order), BF16),
+            pltpu.VMEM((order, bn), BF16),
+            pltpu.SemaphoreType.DMA((6, blocks * n_col)),
+            pltpu.SemaphoreType.DMA((blocks * n_col,)),
+            pltpu.SemaphoreType.DMA((6, blocks)),
+            pltpu.SemaphoreType.DMA((blocks,)),
+            pltpu.SemaphoreType.DMA((2, n_col)),
+            pltpu.SemaphoreType.DMA((n_col,)),
+        ],
+        compiler_params=pltpu.CompilerParams(
+            collective_id=0, has_side_effects=True, vmem_limit_bytes=60 << 20
+        ),
+    )(start.astype(BF16), flags)
+
+
 def solution(mesh):
     placed = (P(("row", "layer"), "col"), P(), P(), P(), P())
     return jax.shard_map(

time: 258 us -> 142 us (0.55)
  the two profiles are of different devices: /device:TPU:6 before, /device:TPU:0 now
where the time goes in v1:
time: 142 us; the launch traced here: 141 us
  Pallas kernels  134 us (94%)
  local copies, waits for them, and re-layouts  2.76 us (2%)
  matrix products  2.34 us (2%)
  between operations  1.98 us (1%)
    pallas_call x1, Pallas kernels, shards(): pl.pallas_call(functools.partial(kernel, (n_row, n_col, n_layer, bm, bn))...  134 us

profile of v1, /device:TPU:0, one launch (start us, length us, event | category | flops | bytes accessed | tf_op | source)
XLA Modules:
  0.0 141.3 jit_solution(15258039787584422528)
XLA Ops:
  1.9 0.0 copy-start.1
  2.0 0.7 copy-done.1
  2.7 0.2 convolution_convert_fusion.flags
  2.9 0.0 copy-start
  2.9 2.1 %fusion.cur = bf16[320,640]{1,0:T(8,128)(2,1)} fusion(bf16[320,20]{1,0:T(8,128)(2,1)S(1)} %convolution_convert_fusion.flags, bf16[320,640]{1,0:T(8,128)(2,1)} %param.5, f32[]{:T(128)} %bitcast.4, f32[]{:T(128)} %bitcast.5, f32[]{:T(128)} %bitcast, s32[640]{0:T(1024)S(1)} %get-tuple-element.8, s32[320]{0:T(512)S(1)} %get-tuple-element.6, ...), kind=kOutput, calls=%fused_computation.1 | convolution fusion | flops 10048000 | bytes 838412 | tf_op jit(solution)/shard_map/dot_general | solution.py:317
  5.0 0.0 copy-done
  5.0 134.2 %shard_map.55 = f32[320,640]{1,0:T(8,128)} custom-call(bf16[320,640]{1,0:T(8,128)(2,1)} %fusion.cur, bf16[320,20]{1,0:T(8,128)(2,1)} %copy-done), custom_call_target="tpu_custom_call" | custom-call | tf_op jit(solution)/shard_map/pallas_call | solution.py:322
  139.2 2.1 %copy.12 = f32[320,640]{1,0:T(8,128)} copy(f32[320,640]{1,0:T(8,128)} %shard_map.55) | data formatting | bytes 1638400
  (2 shorter events, 0.0 us)
Async XLA Ops:
  1.9 0.7 copy-start.1
  2.9 2.1 %copy-start = (bf16[320,20]{1,0:T(8,128)(2,1)}, bf16[320,20]{1,0:T(8,128)(2,1)S(1)}, u32[]{:S(2)}) copy-start(bf16[320,20]{1,0:T(8,128)(2,1)S(1)} %convolution_convert_fusion.flags) | copy-start | bytes 38404

commit v2 on v1

--- a/solution.py
+++ b/solution.py
@@ -198,9 +198,6 @@
     for l in range(n_layer):
         for b in range(n_col):
             g.arrive(None, (row_c, l, b))
-        for b in range(bands):
-            g.arrive(None, (row_yc, l, (1 - y) * bands + b))
-    g.drain()
 
     mine_at = pl.multiple_of(y * half_order, half_order)
     other_at = pl.multiple_of((1 - y) * half_order, half_order)
@@ -210,6 +207,9 @@
         here = pl.ds(pl.multiple_of(mine_at + t * TILE, TILE), TILE)
         full[pl.ds(other_at, half_order), here] = full[here, pl.ds(other_at, half_order)].T
 
+    for l in range(n_layer):
+        for b in range(bands):
+            g.arrive(None, (row_yc, l, (1 - y) * bands + b))
     own_rows = rows_of(row, layer)
 
     def mask_of(b):
@@ -224,9 +224,11 @@
         square[:, cols_of(b)] = value
         half[:, cols_of(b)] = value.astype(BF16)
 
+    cut = bn // 2 // TILE * TILE
+    chunks = ((0, cut), (cut, bn - cut)) if cut else ((0, bn),)
     c = Gather(
-        lambda r, l: column.at[rows_of(r, l), :],
-        lambda r, l: r * n_layer + l,
+        lambda r, l, h: column.at[rows_of(r, l), pl.ds(*chunks[h])],
+        lambda r, l, h: (r * n_layer + l) * 2 + h,
         send2,
         recv2,
     )
@@ -246,34 +248,42 @@
     first = cube_band(z)
     column[own_rows, :] = first
     strip[:, cols_of(z)] = first
-    spread_column(None, (row, layer), True, True)
+    for h in range(len(chunks)):
+        spread_column(None, (row, layer, h), True, True)
 
     @pl.loop(1, n_col)
     def _(i):
         b = lax.rem(z + i, n_col)
         strip[:, cols_of(b)] = cube_band(b)
 
-    for e in range(1, n_layer):
-        for sign in (-1, 1):
-            l = layer + sign * e
-            inside = l >= 0 if sign < 0 else l < n_layer
-            c.arrive(inside, (row, l))
-            spread_column(inside, (row, l), sign < 0, sign > 0)
-    for l in range(n_layer):
-        c.arrive(None, (row_y, l))
-        c.start(None, TO_CORE, (row_y, l), {"row": row_c})
-    for l in range(n_layer):
-        c.arrive(None, (row_c, l))
-    for l in range(n_layer):
-        c.arrive(None, (row_yc, l))
-
+    s = Gather(
+        lambda b, h: half2.at[:, pl.ds(pl.multiple_of(b * bn + chunks[h][0], TILE), chunks[h][1])],
+        lambda b, h: b * 2 + h,
+        send3,
+        recv3,
+    )
     mask_z = mask_of(z)
-    last = mask_z * jnp.dot(strip[...], column[...], preferred_element_type=F32)
-    out[...] = 3.0 * last
-    half2[:, cols_of(z)] = last.astype(BF16)
-    s = Gather(lambda b: half2.at[:, cols_of(b)], lambda b: b, send3, recv3)
-    s.start(z < n_col - 1, Z_UP, (z,), {"col": z + 1})
-    s.start(z > 0, Z_DOWN, (z,), {"col": z - 1})
+    for h in range(len(chunks)):
+        for e in range(1, n_layer):
+            for sign in (-1, 1):
+                l = layer + sign * e
+                inside = l >= 0 if sign < 0 else l < n_layer
+                c.arrive(inside, (row, l, h))
+                spread_column(inside, (row, l, h), sign < 0, sign > 0)
+    for h, (at, width) in enumerate(chunks):
+        for l in range(n_layer):
+            c.arrive(None, (row_y, l, h))
+            c.start(None, TO_CORE, (row_y, l, h), {"row": row_c})
+        for l in range(n_layer):
+            c.arrive(None, (row_c, l, h))
+        for l in range(n_layer):
+            c.arrive(None, (row_yc, l, h))
+        here = slice(at, at + width)
+        last = mask_z[:, here] * jnp.dot(strip[...], column[:, here], preferred_element_type=F32)
+        out[:, here] = 3.0 * last
+        half2[:, pl.ds(pl.multiple_of(z * bn + at, TILE), width)] = last.astype(BF16)
+        s.start(z < n_col - 1, Z_UP, (z, h), {"col": z + 1})
+        s.start(z > 0, Z_DOWN, (z, h), {"col": z - 1})
 
     def cube_part(b):
         part = jnp.dot(half2[:, cols_of(b)], column[cols_of(b), :], preferred_element_type=F32)
@@ -284,17 +294,19 @@
         for sign in (-1, 1):
             b = z + sign * d
             inside = b >= 0 if sign < 0 else b < n_col
-            s.arrive(inside, (b,))
-            if sign < 0:
-                s.start(both(inside, z < n_col - 1), Z_UP, (b,), {"col": z + 1})
-            else:
-                s.start(both(inside, z > 0), Z_DOWN, (b,), {"col": z - 1})
+            for h in range(len(chunks)):
+                s.arrive(inside, (b, h))
+                if sign < 0:
+                    s.start(both(inside, z < n_col - 1), Z_UP, (b, h), {"col": z + 1})
+                else:
+                    s.start(both(inside, z > 0), Z_DOWN, (b, h), {"col": z - 1})
         for sign in (-1, 1):
             b = z + sign * d
             inside = b >= 0 if sign < 0 else b < n_col
             always(inside, functools.partial(cube_part, b))
     s.drain()
     c.drain()
+    g.drain()
 
 
 def shards(hamiltonian, tile_pattern, n_occ, mu, gamma):
@@ -333,10 +345,10 @@
             pltpu.VMEM((order, bn), BF16),
             pltpu.SemaphoreType.DMA((6, blocks * n_col)),
             pltpu.SemaphoreType.DMA((blocks * n_col,)),
-            pltpu.SemaphoreType.DMA((6, blocks)),
-            pltpu.SemaphoreType.DMA((blocks,)),
-            pltpu.SemaphoreType.DMA((2, n_col)),
-            pltpu.SemaphoreType.DMA((n_col,)),
+            pltpu.SemaphoreType.DMA((6, blocks * 2)),
+            pltpu.SemaphoreType.DMA((blocks * 2,)),
+            pltpu.SemaphoreType.DMA((2, n_col * 2)),
+            pltpu.SemaphoreType.DMA((n_col * 2,)),
         ],
         compiler_params=pltpu.CompilerParams(
             collective_id=0, has_side_effects=True, vmem_limit_bytes=60 << 20

time: 142 us -> 134 us (0.944)
  the two profiles are of different devices: /device:TPU:0 before, /device:TPU:6 now
where the time goes in v2:
time: 134 us; the launch traced here: 133 us
  Pallas kernels  126 us (94%)
  local copies, waits for them, and re-layouts  2.76 us (2%)
  matrix products  2.34 us (2%)
  between operations  1.98 us (1%)
    pallas_call x1, Pallas kernels, shards(): pl.pallas_call(functools.partial(kernel, (n_row, n_col, n_layer, bm, bn))...  126 us
    unnamed x5, local copies, waits for them, and re-layouts  2.76 us

profile of v2, /device:TPU:6, one launch (start us, length us, event | category | flops | bytes accessed | tf_op | source)
XLA Modules:
  0.0 133.2 jit_solution(14313820447860005547)
XLA Ops:
  1.9 0.0 copy-start.1
  2.0 0.7 copy-done.1
  2.7 0.2 convolution_convert_fusion.flags
  2.9 0.0 copy-start
  2.9 2.1 %fusion.cur = bf16[320,640]{1,0:T(8,128)(2,1)} fusion(bf16[320,20]{1,0:T(8,128)(2,1)S(1)} %convolution_convert_fusion.flags, bf16[320,640]{1,0:T(8,128)(2,1)} %param.5, f32[]{:T(128)} %bitcast.4, f32[]{:T(128)} %bitcast.5, f32[]{:T(128)} %bitcast, s32[640]{0:T(1024)S(1)} %get-tuple-element.8, s32[320]{0:T(512)S(1)} %get-tuple-element.6, ...), kind=kOutput, calls=%fused_computation.1 | convolution fusion | flops 10048000 | bytes 838412 | tf_op jit(solution)/shard_map/dot_general | solution.py:329
  5.0 0.0 copy-done
  5.0 126.1 %shard_map.55 = f32[320,640]{1,0:T(8,128)} custom-call(bf16[320,640]{1,0:T(8,128)(2,1)} %fusion.cur, bf16[320,20]{1,0:T(8,128)(2,1)} %copy-done), custom_call_target="tpu_custom_call" | custom-call | tf_op jit(solution)/shard_map/pallas_call | solution.py:334
  131.2 2.1 %copy.12 = f32[320,640]{1,0:T(8,128)} copy(f32[320,640]{1,0:T(8,128)} %shard_map.55) | data formatting | bytes 1638400
  (2 shorter events, 0.0 us)
Async XLA Ops:
  1.9 0.7 copy-start.1
  2.9 2.1 %copy-start = (bf16[320,20]{1,0:T(8,128)(2,1)}, bf16[320,20]{1,0:T(8,128)(2,1)S(1)}, u32[]{:S(2)}) copy-start(bf16[320,20]{1,0:T(8,128)(2,1)S(1)} %convolution_convert_fusion.flags) | copy-start | bytes 38404

commit v3 on v2

--- a/solution.py
+++ b/solution.py
@@ -98,6 +98,9 @@
     def rows_of(r, l):
         return pl.ds(pl.multiple_of((r * n_layer + l) * bm, bm), bm)
 
+    def part_of(r, l, h):
+        return pl.ds(pl.multiple_of((r * n_layer + l) * bm + h * (bm // 2), bm // 2), bm // 2)
+
     def cols_of(b):
         return pl.ds(pl.multiple_of(b * bn, bn), bn)
 
@@ -143,14 +146,14 @@
                 always(cond, lambda: self.copy(way, block, device, src).wait_send())
 
     g = Gather(
-        lambda r, l, b: full.at[rows_of(r, l), cols_of(b)],
-        lambda r, l, b: (r * n_layer + l) * n_col + b,
+        lambda r, l, b, h: full.at[part_of(r, l, h), cols_of(b)],
+        lambda r, l, b, h: ((r * n_layer + l) * n_col + b) * 2 + h,
         send1,
         recv1,
     )
 
     def spread(cond, block, up, down, src=None):
-        r, l, b = block
+        b = block[2]
         if up:
             g.start(both(cond, layer < n_layer - 1), L_UP, block, {"layer": layer + 1}, src)
         if down:
@@ -158,10 +161,12 @@
         g.start(both(cond, b // bands == y), TO_Y, block, {"row": row_y}, src)
         g.start(cond, TO_CORE, block, {"row": row_c}, src)
 
-    mine = (row, layer, z)
-    g.start(z < n_col - 1, Z_UP, mine, {"col": z + 1}, cur)
-    g.start(z > 0, Z_DOWN, mine, {"col": z - 1}, cur)
-    spread(None, mine, True, True, cur)
+    for h in range(2):
+        mine = (row, layer, z, h)
+        piece = cur.at[pl.ds(h * (bm // 2), bm // 2), :]
+        g.start(z < n_col - 1, Z_UP, mine, {"col": z + 1}, piece)
+        g.start(z > 0, Z_DOWN, mine, {"col": z - 1}, piece)
+        spread(None, mine, True, True, piece)
     full[rows_of(row, layer), cols_of(z)] = cur[...]
 
     def layer_arrivals(cond, b):
@@ -169,20 +174,22 @@
             for sign in (-1, 1):
                 l = layer + sign * e
                 inside = both(cond, l >= 0 if sign < 0 else l < n_layer)
-                g.arrive(inside, (row, l, b))
-                spread(inside, (row, l, b), sign < 0, sign > 0)
+                for h in range(2):
+                    g.arrive(inside, (row, l, b, h))
+                    spread(inside, (row, l, b, h), sign < 0, sign > 0)
 
     for d in range(1, n_col):
         for sign in (-1, 1):
             b = z + sign * d
             inside = b >= 0 if sign < 0 else b < n_col
-            block = (row, layer, b)
-            g.arrive(inside, block)
-            if sign < 0:
-                g.start(both(inside, z < n_col - 1), Z_UP, block, {"col": z + 1})
-            else:
-                g.start(both(inside, z > 0), Z_DOWN, block, {"col": z - 1})
-            spread(inside, block, True, True)
+            for h in range(2):
+                block = (row, layer, b, h)
+                g.arrive(inside, block)
+                if sign < 0:
+                    g.start(both(inside, z < n_col - 1), Z_UP, block, {"col": z + 1})
+                else:
+                    g.start(both(inside, z > 0), Z_DOWN, block, {"col": z - 1})
+                spread(inside, block, True, True)
         if d == 1:
             layer_arrivals(None, z)
         else:
@@ -192,12 +199,14 @@
     layer_arrivals(z + n_col - 1 < n_col, z + n_col - 1)
     for b in range(bands):
         for l in range(n_layer):
-            block = (row_y, l, (1 - y) * bands + b)
-            g.arrive(None, block)
-            g.start(None, TO_CORE, block, {"row": row_c})
+            for h in range(2):
+                block = (row_y, l, (1 - y) * bands + b, h)
+                g.arrive(None, block)
+                g.start(None, TO_CORE, block, {"row": row_c})
     for l in range(n_layer):
         for b in range(n_col):
-            g.arrive(None, (row_c, l, b))
+            for h in range(2):
+                g.arrive(None, (row_c, l, b, h))
 
     mine_at = pl.multiple_of(y * half_order, half_order)
     other_at = pl.multiple_of((1 - y) * half_order, half_order)
@@ -209,7 +218,8 @@
 
     for l in range(n_layer):
         for b in range(bands):
-            g.arrive(None, (row_yc, l, (1 - y) * bands + b))
+            for h in range(2):
+                g.arrive(None, (row_yc, l, (1 - y) * bands + b, h))
     own_rows = rows_of(row, layer)
 
     def mask_of(b):
@@ -315,7 +325,7 @@
     order = bn * n_col
     vmem = 2 * order * (order + 3 * bm + bn) + 4 * bm * (order + bn) + 2 * bm * bn
     regular = n_row == 4 and n_col % 2 == 0 and n_layer * bm * n_row == order
-    aligned = bm % 16 == 0 and bn % TILE == 0 and (order // 2) % TILE == 0
+    aligned = bm % 32 == 0 and bn % TILE == 0 and (order // 2) % TILE == 0
     if not (regular and aligned and vmem <= 48 << 20):
         return plain_shards(hamiltonian, tile_pattern, n_occ, mu, gamma)
     row_start = (lax.axis_index("row") * n_layer + lax.axis_index("layer")) * bm
@@ -343,8 +353,8 @@
             pltpu.VMEM((bm, order), BF16),
             pltpu.VMEM((bm, order), BF16),
             pltpu.VMEM((order, bn), BF16),
-            pltpu.SemaphoreType.DMA((6, blocks * n_col)),
-            pltpu.SemaphoreType.DMA((blocks * n_col,)),
+            pltpu.SemaphoreType.DMA((6, blocks * n_col * 2)),
+            pltpu.SemaphoreType.DMA((blocks * n_col * 2,)),
             pltpu.SemaphoreType.DMA((6, blocks * 2)),
             pltpu.SemaphoreType.DMA((blocks * 2,)),
             pltpu.SemaphoreType.DMA((2, n_col * 2)),

time: 134 us -> 130 us (0.970)
  Pallas kernels: 126 us -> 123 us
    pallas_call x1, Pallas kernels: 126 us -> 123 us  [shards(): pl.pallas_call(functools.partial(kernel, (n_row, n_col, n_layer, bm, bn))...]
where the time goes in v3:
time: 130 us
  Pallas kernels  123 us (95%)
  local copies, waits for them, and re-layouts  2.76 us (2%)
  matrix products  2.34 us (2%)
  between operations  1.98 us (2%)
    pallas_call x1, Pallas kernels, shards(): pl.pallas_call(functools.partial(kernel, (n_row, n_col, n_layer, bm, bn))...  123 us
    unnamed x5, local copies, waits for them, and re-layouts  2.76 us

profile of v3, /device:TPU:6, one launch (start us, length us, event | category | flops | bytes accessed | tf_op | source)
XLA Modules:
  0.0 129.8 jit_solution(13500889621149868498)
XLA Ops:
  1.9 0.0 copy-start.1
  2.0 0.7 copy-done.1
  2.7 0.2 convolution_convert_fusion.flags
  2.9 0.0 copy-start
  2.9 2.1 %fusion.cur = bf16[320,640]{1,0:T(8,128)(2,1)} fusion(bf16[320,20]{1,0:T(8,128)(2,1)S(1)} %convolution_convert_fusion.flags, bf16[320,640]{1,0:T(8,128)(2,1)} %param.5, f32[]{:T(128)} %bitcast.4, f32[]{:T(128)} %bitcast.5, f32[]{:T(128)} %bitcast, s32[640]{0:T(1024)S(1)} %get-tuple-element.8, s32[320]{0:T(512)S(1)} %get-tuple-element.6, ...), kind=kOutput, calls=%fused_computation.1 | convolution fusion | flops 10048000 | bytes 838412 | tf_op jit(solution)/shard_map/dot_general | solution.py:339
  5.0 0.0 copy-done
  5.0 122.6 %shard_map.55 = f32[320,640]{1,0:T(8,128)} custom-call(bf16[320,640]{1,0:T(8,128)(2,1)} %fusion.cur, bf16[320,20]{1,0:T(8,128)(2,1)} %copy-done), custom_call_target="tpu_custom_call" | custom-call | tf_op jit(solution)/shard_map/pallas_call | solution.py:344
  127.7 2.1 %copy.12 = f32[320,640]{1,0:T(8,128)} copy(f32[320,640]{1,0:T(8,128)} %shard_map.55) | data formatting | bytes 1638400
  (2 shorter events, 0.0 us)
Async XLA Ops:
  1.9 0.7 copy-start.1
  2.9 2.1 %copy-start = (bf16[320,20]{1,0:T(8,128)(2,1)}, bf16[320,20]{1,0:T(8,128)(2,1)S(1)}, u32[]{:S(2)}) copy-start(bf16[320,20]{1,0:T(8,128)(2,1)S(1)} %convolution_convert_fusion.flags) | copy-start | bytes 38404
